TPU v7x, 32 devices: a 4x4x1 block of a 4x4x8 slice. The times are simulated.
32 devices in a mesh: rep: 2 (over z, core), dp: 16 (over x, y).
Axes of the slice: x: 4, y: 4, z: 1, core: 2. Of those that a mesh axis runs over, the one named last changes fastest.
The devices are a block of a 4x4x8 slice.
Arguments:
- a: bfloat16 [32, 4, 4096, 640], P(('rep', 'dp')), parts along dimension 0
- g: bfloat16 [32, 4, 4096, 3200], P(('rep', 'dp')), parts along dimension 0
Outputs:
- output: bfloat16 [8, 640, 3200], P('rep'), parts along dimension 0
There are 2 independent parts. A program takes and returns all parts, laid end to end along the dimension named above; each array names one.
All inputs are finite; a program needn't handle non-finite values.
Results may differ from a plain program's by a relative error of at most 0.012.
Values are sent between devices in bfloat16 or wider.
A program may use at most 768 MiB of HBM per device.

v0:
```python
import jax
import jax.numpy as jnp


def solution(mesh):
    groups = mesh.shape["rep"]

    def step(a, g):
        a, g = (t.reshape(groups, -1, *t.shape[1:]) for t in (a, g))
        sums = jnp.einsum("rsntd,rsntf->rndf", a, g, preferred_element_type=jnp.float32)
        return sums.astype(jnp.bfloat16).reshape(-1, *sums.shape[2:])

    return step
```

profile of v0, /device:TPU:96, one launch (start us, length us, event | category | flops | bytes accessed | tf_op | source)
XLA Modules:
  0.0 790.8 jit_solution(7963383386073394115)
XLA Ops:
  0.0 86.8 %fusion.3 = f32[1,4,640,3200]{3,2,1,0:T(8,128)} fusion(bf16[1,4,4096,3200]{3,2,1,0:T(8,128)(2,1)} %param.1, bf16[1,4,4096,640]{3,2,1,0:T(8,128)(2,1)} %param), kind=kOutput, calls=%fused_computation.4 | convolution fusion | flops 67108864000 | bytes 158597120 | tf_op jit(solution)/rsntd,rsntf->rndf/dot_general | solution.py:10
  86.8 704.0 %all-reduce.2 = bf16[1,4,640,3200]{3,2,1,0:T(8,128)(2,1)} all-reduce(f32[1,4,640,3200]{3,2,1,0:T(8,128)} %fusion.3), channel_id=1, replica_groups=[2,16]<=[32], use_global_device_ids=true, to_apply=%add.clone | all-reduce | flops 8192000 | bytes 49152000 | tf_op jit(solution)/rsntd,rsntf->rndf/dot_general | solution.py:10
where the time goes:
time: 791 us
  blocking collectives  704 us (89%)
  matrix products  86.8 us (11%)
    dot_general x1, blocking collectives, step(): jnp.einsum('rsntd,rsntf->rndf', a, g, preferred_element_type=jnp.float32)  704 us
    dot_general x1, matrix products, step(): jnp.einsum('rsntd,rsntf->rndf', a, g, preferred_element_type=jnp.float32)  86.8 us

commit v1 on v0

v1 whole, which is shorter than its diff:
```python
import functools
import math

import jax
import jax.numpy as jnp
from jax import lax
from jax.experimental import pallas as pl
from jax.experimental.pallas import tpu as pltpu
from jax.sharding import PartitionSpec as P

MESH = pl.DeviceIdType.MESH
LANE = 128
ACC = 6
RING = 8
SENT = 2
BF = jnp.bfloat16
F32 = jnp.float32


def kernel(
    side, a_hbm, g_hbm, out,
    abuf, gbuf, xbuf, acc,
    s0, s1, s2p, s2m, s3,
    r0, r1, r2p, r2m, r3,
    asem, gsem, xsem, send_sem, recv_sem, credit,
):
    mats, tokens, rows = a_hbm.shape
    cols = g_hbm.shape[2]
    chunk = side * LANE
    per = cols // chunk
    whole = mats * per
    total = whole + 1
    half = rows // 2
    band = half // side
    hc = chunk // 2
    up, down = s2p.shape[2], s2m.shape[2]

    me = lax.axis_index("dp")
    ix, iy = me // side, me % side

    def at(x, y):
        return {"dp": lax.rem(x + side, side) * side + lax.rem(y + side, side)}

    near = [[at(ix + 1, iy), at(ix - 1, iy)], [at(ix, iy + 1), at(ix, iy - 1)]]
    pos = [ix, iy]

    def ring(v):
        return lax.rem(v + side, side)

    def load_a(n):
        return pltpu.make_async_copy(a_hbm.at[n], abuf.at[n % 2], asem.at[n % 2])

    def load_g(q):
        n, c = q // per, q % per
        return pltpu.make_async_copy(
            g_hbm.at[n, :, pl.ds(pl.multiple_of(c * chunk, LANE), chunk)], gbuf.at[q % 2], gsem.at[q % 2]
        )

    def load_x(n):
        return pltpu.make_async_copy(g_hbm.at[n, :, pl.ds(per * chunk, LANE)], xbuf, xsem)

    load_a(0).start()
    load_g(0).start()
    load_g(1).start()
    load_x(0).start()

    barrier = pltpu.get_barrier_semaphore()
    for axis in range(2):
        for d in range(2):
            pl.semaphore_signal(barrier, inc=1, device_id=near[axis][d], device_id_type=MESH)
    pl.semaphore_wait(barrier, 4)

    def aslot(q):
        return jnp.where(q == whole, ACC, q % ACC)

    def row0(c, k):
        return pl.multiple_of(c * half + k * band, 16)

    def lane0(l):
        return pl.multiple_of(l * LANE, LANE)

    def piece(q, c, k, l, r0_=0, n=None):
        return out.at[q, pl.ds(row0(c, k) + r0_, band if n is None else n), pl.ds(lane0(l), LANE)]

    def remote(s, q, c, d):
        first, second = c, 1 - c
        p1, p2 = pos[first], pos[second]
        axis = first if s in (0, 1, 6, 7) else second
        w, r = q % SENT, q % RING
        if s == 0:
            src, dst = s0.at[c, d, w], r0.at[c, d, r]
        elif s == 1:
            src, dst = s1.at[c, d, w], r1.at[c, d, r]
        elif s == 2:
            src, dst = (s2p.at[c, w], r2p.at[c, r]) if d == 0 else (s2m.at[c, w], r2m.at[c, r])
        elif s == 3:
            src, dst = s3.at[c, d, w], r3.at[c, d, r]
        elif s == 4:
            src = dst = piece(q, c, p1, p2)
        elif s == 5:
            if d == 0:
                src = dst = piece(q, c, p1, ring(p2 - 1), 0, down)
            else:
                src = dst = piece(q, c, p1, ring(p2 + 1), down, up)
        elif s == 6:
            src = dst = out.at[q, pl.ds(row0(c, p1), band), :]
        else:
            k = ring(p1 - 1) if d == 0 else ring(p1 + 1)
            src = dst = out.at[q, pl.ds(row0(c, k), band), pl.ds(d * hc, hc)]
        return pltpu.make_async_remote_copy(
            src_ref=src, dst_ref=dst,
            send_sem=send_sem.at[s, c, d, w], recv_sem=recv_sem.at[s, c, d, r],
            device_id=near[axis][d], device_id_type=MESH,
        )

    def reuse(s, q, c, d):
        @pl.when(q >= SENT)
        def _():
            remote(s, q, c, d).wait_send()

    def first_sends(q, d):
        slot = aslot(q)
        for c in range(2):
            reuse(0, q, c, d)
            k = ring(pos[c] + 2)
            s0[c, d, q % SENT] = acc[slot, pl.ds(row0(c, k), band), pl.ds(d * hc, hc)].astype(BF)
            remote(0, q, c, d).start()

    def step1(q):
        slot = aslot(q)
        for d in range(2):
            for c in range(2):
                remote(0, q, c, d).wait_recv()
                reuse(1, q, c, d)
                k = ring(pos[c] + (1 if d == 0 else -1))
                r = pl.ds(row0(c, k), band)
                w = q % SENT
                mine, other = pl.ds(d * hc, hc), pl.ds((1 - d) * hc, hc)
                s1[c, d, w, :, mine] = (acc[slot, r, mine] + r0[c, d, q % RING].astype(F32)).astype(BF)
                s1[c, d, w, :, other] = acc[slot, r, other].astype(BF)
                remote(1, q, c, d).start()

    def summed(q, c, l, r0_, n):
        z, lanes = q % RING, pl.ds(lane0(l), LANE)
        v = acc[aslot(q), pl.ds(row0(c, pos[c]) + r0_, n), lanes]
        rs = pl.ds(r0_, n)
        return v + r1[c, 0, z, rs, lanes].astype(F32) + r1[c, 1, z, rs, lanes].astype(F32)

    def step2(q):
        for c in range(2):
            for d in range(2):
                remote(1, q, c, d).wait_recv()
            l = ring(pos[1 - c] + 2)
            w = q % SENT
            for d in range(2):
                reuse(2, q, c, d)
                if d == 0:
                    s2p[c, w] = summed(q, c, l, 0, up).astype(BF)
                else:
                    s2m[c, w] = summed(q, c, l, up, down).astype(BF)
                remote(2, q, c, d).start()

    def step3(q):
        for d in range(2):
            for c in range(2):
                remote(2, q, c, d).wait_recv()
                reuse(3, q, c, d)
                l = ring(pos[1 - c] + (1 if d == 0 else -1))
                w, z = q % SENT, q % RING
                top, low = summed(q, c, l, 0, up), summed(q, c, l, up, down)
                if d == 0:
                    top = top + r2p[c, z].astype(F32)
                else:
                    low = low + r2m[c, z].astype(F32)
                s3[c, d, w, pl.ds(0, up)] = top.astype(BF)
                s3[c, d, w, pl.ds(up, down)] = low.astype(BF)
                remote(3, q, c, d).start()

    def step4(q):
        z = q % RING
        for c in range(2):
            for d in range(2):
                remote(3, q, c, d).wait_recv()
            v = summed(q, c, pos[1 - c], 0, band) + r3[c, 0, z].astype(F32) + r3[c, 1, z].astype(F32)
            out[q, pl.ds(row0(c, pos[c]), band), pl.ds(lane0(pos[1 - c]), LANE)] = v.astype(BF)
            for d in range(2):
                reuse(4, q, c, d)
                remote(4, q, c, d).start()

        @pl.when(q + RING < total)
        def _():
            for axis in range(2):
                for d in range(2):
                    pl.semaphore_signal(
                        credit.at[axis, d], inc=1, device_id=near[axis][d], device_id_type=MESH
                    )

    def arrived(s, q, c, d):
        first, second = c, 1 - c
        p1, p2 = pos[first], pos[second]
        back = -1 if d == 0 else 1
        if s == 4:
            dst = piece(q, c, p1, ring(p2 + back))
        elif s == 5:
            dst = piece(q, c, p1, ring(p2 + 2), 0, down) if d == 0 else piece(q, c, p1, ring(p2 + 2), down, up)
        elif s == 6:
            dst = out.at[q, pl.ds(row0(c, ring(p1 + back)), band), :]
        else:
            dst = out.at[q, pl.ds(row0(c, ring(p1 + 2)), band), pl.ds(d * hc, hc)]
        axis = second if s in (4, 5) else first
        pltpu.make_async_remote_copy(
            src_ref=dst, dst_ref=dst,
            send_sem=send_sem.at[s, c, d, q % SENT], recv_sem=recv_sem.at[s, c, d, q % RING],
            device_id=near[axis][d], device_id_type=MESH,
        ).wait_recv()

    def step5(q):
        for d in range(2):
            for c in range(2):
                arrived(4, q, c, d)
                reuse(5, q, c, d)
                remote(5, q, c, d).start()

    def step6(q):
        for c in range(2):
            for d in range(2):
                arrived(5, q, c, d)
            for d in range(2):
                reuse(6, q, c, d)
                remote(6, q, c, d).start()

    def step7(q):
        for d in range(2):
            for c in range(2):
                arrived(6, q, c, d)
                reuse(7, q, c, d)
                remote(7, q, c, d).start()

    def step8(q):
        for d in range(2):
            for c in range(2):
                arrived(7, q, c, d)

    def dot(n, w):
        return lax.dot_general(abuf[n % 2], w, (((0,), (0,)), ((), ())), preferred_element_type=F32)

    def stage(t, s, f):
        @pl.when((t >= s) & (t < total + s))
        def _():
            f(t - s)

    def turn(t, carry):
        n, c = t // per, t % per

        @pl.when(t < whole)
        def _():
            @pl.when(c == 0)
            def _():
                load_a(n).wait()

                @pl.when(n + 1 < mats)
                def _():
                    load_a(n + 1).start()

            load_g(t).wait()
            acc[t % ACC, :, pl.ds(0, hc)] = dot(n, gbuf[t % 2, :, pl.ds(0, hc)])

        @pl.when((t >= RING) & (t < total))
        def _():
            for axis in range(2):
                for d in range(2):
                    pl.semaphore_wait(credit.at[axis, d], 1)

        @pl.when(t < total)
        def _():
            first_sends(t, 0)

        stage(t, 1, step1)
        stage(t, 2, step2)
        stage(t, 3, step3)
        stage(t, 4, step4)

        @pl.when(t < whole)
        def _():
            acc[t % ACC, :, pl.ds(hc, hc)] = dot(n, gbuf[t % 2, :, pl.ds(hc, hc)])

            @pl.when(t + 2 < whole)
            def _():
                load_g(t + 2).start()

        @pl.when(t < total)
        def _():
            first_sends(t, 1)

        stage(t, 5, step5)
        stage(t, 6, step6)

        @pl.when((t < whole) & (c == per - 1))
        def _():
            load_x(n).wait()
            acc[ACC, :, pl.ds(lane0(n), LANE)] = dot(n, xbuf[...])

            @pl.when(n + 1 < mats)
            def _():
                load_x(n + 1).start()

        stage(t, 7, step7)
        stage(t, 8, step8)
        return carry

    lax.fori_loop(0, total + 8, turn, 0)

    for s in range(8):
        for c in range(2):
            for d in range(2):
                for k in range(SENT):
                    remote(s, total - SENT + k, c, d).wait_send()


def write(per, sums, out, sem):
    mats = out.shape[0]
    chunk = sums.shape[2]
    copies = []
    for n in range(mats):
        for c in range(per):
            copies.append((sums.at[n * per + c], out.at[n, :, pl.ds(c * chunk, chunk)]))
        copies.append((sums.at[mats * per, :, pl.ds(n * LANE, LANE)], out.at[n, :, pl.ds(per * chunk, LANE)]))
    copies = [pltpu.make_async_copy(s, d, sem.at[i]) for i, (s, d) in enumerate(copies)]
    for copy in copies:
        copy.start()
    for copy in copies:
        copy.wait()


def solution(mesh):
    side = math.isqrt(mesh.shape["dp"])

    def step(a, g):
        a, g = a[0], g[0]
        mats, tokens, rows = a.shape
        cols = g.shape[2]
        chunk = side * LANE
        per = cols // chunk
        total = mats * per + 1
        band, hc = rows // 2 // side, chunk // 2
        up = (band // 2 + 15) // 16 * 16
        down = band - up
        dma = pltpu.SemaphoreType.DMA
        sums = pl.pallas_call(
            functools.partial(kernel, side),
            out_shape=pltpu.VMEM((total, rows, chunk), BF),
            in_specs=[pl.BlockSpec(memory_space=pl.ANY)] * 2,
            out_specs=pl.BlockSpec(memory_space=pltpu.VMEM),
            scratch_shapes=[
                pltpu.VMEM((2, tokens, rows), BF),
                pltpu.VMEM((2, tokens, chunk), BF),
                pltpu.VMEM((tokens, LANE), BF),
                pltpu.VMEM((ACC + 1, rows, chunk), F32),
                pltpu.VMEM((2, 2, SENT, band, hc), BF),
                pltpu.VMEM((2, 2, SENT, band, chunk), BF),
                pltpu.VMEM((2, SENT, up, LANE), BF),
                pltpu.VMEM((2, SENT, down, LANE), BF),
                pltpu.VMEM((2, 2, SENT, band, LANE), BF),
                pltpu.VMEM((2, 2, RING, band, hc), BF),
                pltpu.VMEM((2, 2, RING, band, chunk), BF),
                pltpu.VMEM((2, RING, up, LANE), BF),
                pltpu.VMEM((2, RING, down, LANE), BF),
                pltpu.VMEM((2, 2, RING, band, LANE), BF),
                dma((2,)),
                dma((2,)),
                dma(()),
                dma((8, 2, 2, SENT)),
                dma((8, 2, 2, RING)),
                pltpu.SemaphoreType.REGULAR((2, 2)),
            ],
            compiler_params=pltpu.CompilerParams(
                collective_id=0, has_side_effects=True, vmem_limit_bytes=45 * 2**20
            ),
        )(a, g)
        return pl.pallas_call(
            functools.partial(write, per),
            out_shape=jax.ShapeDtypeStruct((mats, rows, cols), BF),
            in_specs=[pl.BlockSpec(memory_space=pltpu.VMEM)],
            out_specs=pl.BlockSpec(memory_space=pl.ANY),
            scratch_shapes=[dma((mats * (per + 1),))],
            compiler_params=pltpu.CompilerParams(vmem_limit_bytes=2**20),
        )(sums)

    return jax.shard_map(
        step,
        mesh=mesh,
        in_specs=(P(("rep", "dp")), P(("rep", "dp"))),
        out_specs=P("rep"),
        check_vma=False,
    )
```

time: 791 us -> 202 us (0.26)
  blocking collectives: 704 us -> 0 us
  Pallas kernels: 0 us -> 202 us
  matrix products: 86.8 us -> 0 us
    dot_general x1 -> x0, blocking collectives: 704 us -> none  [step(): jnp.einsum('rsntd,rsntf->rndf', a, g, preferred_element_type=jnp.float32)]
    pallas_call x0 -> x2, Pallas kernels: none -> 202 us  [the longest x1 196 us: step(): pl.pallas_call(functools.partial(kernel, side), out_shape=pltpu.VMEM((tot...]
    dot_general x1 -> x0, matrix products: 86.8 us -> none  [step(): jnp.einsum('rsntd,rsntf->rndf', a, g, preferred_element_type=jnp.float32)]
where the time goes in v1:
time: 202 us
  Pallas kernels  202 us (100%)
    pallas_call x1, Pallas kernels, step(): pl.pallas_call(functools.partial(kernel, side), out_shape=pltpu.VMEM((tot...  196 us
    pallas_call x1, Pallas kernels, step(): pl.pallas_call(functools.partial(write, per), out_shape=jax.ShapeDtypeStr...  5.92 us

profile of v1, /device:TPU:96, one launch (start us, length us, event | category | flops | bytes accessed | tf_op | source)
XLA Modules:
  0.0 201.6 jit_solution(746579894466275210)
XLA Ops:
  0.0 195.7 %shard_map.28.sums = bf16[25,640,512]{2,1,0:T(8,128)(2,1)S(1)} custom-call(bf16[4,4096,640]{2,1,0:T(8,128)(2,1)} %bitcast.2, bf16[4,4096,3200]{2,1,0:T(8,128)(2,1)} %bitcast.1.g_hbm), custom_call_target="tpu_custom_call" | custom-call | tf_op jit(solution)/shard_map/pallas_call | solution.py:349
  195.7 5.9 %shard_map.29 = bf16[4,640,3200]{2,1,0:T(8,128)(2,1)} custom-call(bf16[25,640,512]{2,1,0:T(8,128)(2,1)S(1)} %shard_map.28.sums), custom_call_target="tpu_custom_call" | custom-call | tf_op jit(solution)/shard_map/pallas_call | solution.py:380

commit v2 on v1

--- a/solution.py
+++ b/solution.py
@@ -13,6 +13,8 @@
 ACC = 6
 RING = 8
 SENT = 2
+PARTS = 8
+AHEAD = 3
 BF = jnp.bfloat16
 F32 = jnp.float32
 
@@ -22,7 +24,7 @@
     abuf, gbuf, xbuf, acc,
     s0, s1, s2p, s2m, s3,
     r0, r1, r2p, r2m, r3,
-    asem, gsem, xsem, send_sem, recv_sem, credit,
+    asem, gsem, xsem, psem, send_sem, recv_sem, credit,
 ):
     mats, tokens, rows = a_hbm.shape
     cols = g_hbm.shape[2]
@@ -59,15 +61,51 @@
     def load_x(n):
         return pltpu.make_async_copy(g_hbm.at[n, :, pl.ds(per * chunk, LANE)], xbuf, xsem)
 
-    load_a(0).start()
-    load_g(0).start()
-    load_g(1).start()
-    load_x(0).start()
+    depth = tokens // PARTS
+
+    def first_loads(k):
+        r = pl.ds(pl.multiple_of(k * depth, depth), depth)
+        return (
+            pltpu.make_async_copy(a_hbm.at[0, r, :], abuf.at[0, r, :], psem.at[0, k]),
+            pltpu.make_async_copy(g_hbm.at[0, r, pl.ds(0, chunk)], gbuf.at[0, r, :], psem.at[1, k]),
+        )
+
+    for k in range(AHEAD):
+        for copy in first_loads(k):
+            copy.start()
 
     barrier = pltpu.get_barrier_semaphore()
     for axis in range(2):
         for d in range(2):
             pl.semaphore_signal(barrier, inc=1, device_id=near[axis][d], device_id_type=MESH)
+
+    acc[0] = jnp.zeros(acc.shape[1:], F32)
+
+    def first_dot(k, carry):
+        for copy in first_loads(k):
+            copy.wait()
+
+        @pl.when(k + AHEAD < PARTS)
+        def _():
+            for copy in first_loads(k + AHEAD):
+                copy.start()
+
+        @pl.when(k == PARTS - AHEAD)
+        def _():
+            load_g(1).start()
+
+        r = pl.ds(pl.multiple_of(k * depth, depth), depth)
+        for h in range(2):
+            lanes = pl.ds(h * hc, hc)
+            acc[0, :, lanes] += lax.dot_general(
+                abuf[0, r, :], gbuf[0, r, lanes], (((0,), (0,)), ((), ())), preferred_element_type=F32
+            )
+        return carry
+
+    lax.fori_loop(0, PARTS, first_dot, 0)
+    load_a(1).start()
+    load_g(2).start()
+    load_x(0).start()
     pl.semaphore_wait(barrier, 4)
 
     def aslot(q):
@@ -113,25 +151,28 @@
             device_id=near[axis][d], device_id_type=MESH,
         )
 
-    def reuse(s, q, c, d):
+    def reuse(s, q):
         @pl.when(q >= SENT)
         def _():
-            remote(s, q, c, d).wait_send()
-
-    def first_sends(q, d):
+            for d in range(2):
+                for c in range(2):
+                    remote(s, q, c, d).wait_send()
+
+    def step0(q):
         slot = aslot(q)
-        for c in range(2):
-            reuse(0, q, c, d)
-            k = ring(pos[c] + 2)
-            s0[c, d, q % SENT] = acc[slot, pl.ds(row0(c, k), band), pl.ds(d * hc, hc)].astype(BF)
-            remote(0, q, c, d).start()
+        reuse(0, q)
+        for d in range(2):
+            for c in range(2):
+                k = ring(pos[c] + 2)
+                s0[c, d, q % SENT] = acc[slot, pl.ds(row0(c, k), band), pl.ds(d * hc, hc)].astype(BF)
+                remote(0, q, c, d).start()
 
     def step1(q):
         slot = aslot(q)
+        reuse(1, q)
         for d in range(2):
             for c in range(2):
                 remote(0, q, c, d).wait_recv()
-                reuse(1, q, c, d)
                 k = ring(pos[c] + (1 if d == 0 else -1))
                 r = pl.ds(row0(c, k), band)
                 w = q % SENT
@@ -147,13 +188,13 @@
         return v + r1[c, 0, z, rs, lanes].astype(F32) + r1[c, 1, z, rs, lanes].astype(F32)
 
     def step2(q):
+        reuse(2, q)
         for c in range(2):
             for d in range(2):
                 remote(1, q, c, d).wait_recv()
             l = ring(pos[1 - c] + 2)
             w = q % SENT
             for d in range(2):
-                reuse(2, q, c, d)
                 if d == 0:
                     s2p[c, w] = summed(q, c, l, 0, up).astype(BF)
                 else:
@@ -161,10 +202,10 @@
                 remote(2, q, c, d).start()
 
     def step3(q):
+        reuse(3, q)
         for d in range(2):
             for c in range(2):
                 remote(2, q, c, d).wait_recv()
-                reuse(3, q, c, d)
                 l = ring(pos[1 - c] + (1 if d == 0 else -1))
                 w, z = q % SENT, q % RING
                 top, low = summed(q, c, l, 0, up), summed(q, c, l, up, down)
@@ -177,6 +218,7 @@
                 remote(3, q, c, d).start()
 
     def step4(q):
+        reuse(4, q)
         z = q % RING
         for c in range(2):
             for d in range(2):
@@ -184,7 +226,6 @@
             v = summed(q, c, pos[1 - c], 0, band) + r3[c, 0, z].astype(F32) + r3[c, 1, z].astype(F32)
             out[q, pl.ds(row0(c, pos[c]), band), pl.ds(lane0(pos[1 - c]), LANE)] = v.astype(BF)
             for d in range(2):
-                reuse(4, q, c, d)
                 remote(4, q, c, d).start()
 
         @pl.when(q + RING < total)
@@ -215,25 +256,25 @@
         ).wait_recv()
 
     def step5(q):
+        reuse(5, q)
         for d in range(2):
             for c in range(2):
                 arrived(4, q, c, d)
-                reuse(5, q, c, d)
                 remote(5, q, c, d).start()
 
     def step6(q):
+        reuse(6, q)
         for c in range(2):
             for d in range(2):
                 arrived(5, q, c, d)
             for d in range(2):
-                reuse(6, q, c, d)
                 remote(6, q, c, d).start()
 
     def step7(q):
+        reuse(7, q)
         for d in range(2):
             for c in range(2):
                 arrived(6, q, c, d)
-                reuse(7, q, c, d)
                 remote(7, q, c, d).start()
 
     def step8(q):
@@ -250,59 +291,54 @@
             f(t - s)
 
     def turn(t, carry):
-        n, c = t // per, t % per
-
-        @pl.when(t < whole)
+        u = t + 1
+        n, c = u // per, u % per
+
+        @pl.when((t >= RING) & (t < total))
+        def _():
+            for axis in range(2):
+                for d in range(2):
+                    pl.semaphore_wait(credit.at[axis, d], 1)
+
+        stage(t, 0, step0)
+        stage(t, 1, step1)
+
+        @pl.when(u < whole)
         def _():
             @pl.when(c == 0)
             def _():
                 load_a(n).wait()
 
-                @pl.when(n + 1 < mats)
-                def _():
-                    load_a(n + 1).start()
-
-            load_g(t).wait()
-            acc[t % ACC, :, pl.ds(0, hc)] = dot(n, gbuf[t % 2, :, pl.ds(0, hc)])
-
-        @pl.when((t >= RING) & (t < total))
-        def _():
-            for axis in range(2):
-                for d in range(2):
-                    pl.semaphore_wait(credit.at[axis, d], 1)
-
-        @pl.when(t < total)
-        def _():
-            first_sends(t, 0)
-
-        stage(t, 1, step1)
+            load_g(u).wait()
+            acc[u % ACC, :, pl.ds(0, hc)] = dot(n, gbuf[u % 2, :, pl.ds(0, hc)])
+
         stage(t, 2, step2)
         stage(t, 3, step3)
         stage(t, 4, step4)
 
-        @pl.when(t < whole)
-        def _():
-            acc[t % ACC, :, pl.ds(hc, hc)] = dot(n, gbuf[t % 2, :, pl.ds(hc, hc)])
-
-            @pl.when(t + 2 < whole)
+        @pl.when(u < whole)
+        def _():
+            acc[u % ACC, :, pl.ds(hc, hc)] = dot(n, gbuf[u % 2, :, pl.ds(hc, hc)])
+
+            @pl.when(u + 2 < whole)
             def _():
-                load_g(t + 2).start()
-
-        @pl.when(t < total)
-        def _():
-            first_sends(t, 1)
+                load_g(u + 2).start()
 
         stage(t, 5, step5)
         stage(t, 6, step6)
 
-        @pl.when((t < whole) & (c == per - 1))
-        def _():
-            load_x(n).wait()
-            acc[ACC, :, pl.ds(lane0(n), LANE)] = dot(n, xbuf[...])
+        @pl.when((c == 0) & (u <= whole))
+        def _():
+            load_x(n - 1).wait()
+            acc[ACC, :, pl.ds(lane0(n - 1), LANE)] = dot(n - 1, xbuf[...])
+
+            @pl.when(n < mats)
+            def _():
+                load_x(n).start()
 
             @pl.when(n + 1 < mats)
             def _():
-                load_x(n + 1).start()
+                load_a(n + 1).start()
 
         stage(t, 7, step7)
         stage(t, 8, step8)
@@ -369,6 +405,7 @@
                 dma((2,)),
                 dma((2,)),
                 dma(()),
+                dma((2, PARTS)),
                 dma((8, 2, 2, SENT)),
                 dma((8, 2, 2, RING)),
                 pltpu.SemaphoreType.REGULAR((2, 2)),

time: 202 us -> 197 us (0.975)
  Pallas kernels: 202 us -> 197 us
    pallas_call x1, Pallas kernels: 196 us -> 191 us  [step(): pl.pallas_call(functools.partial(kernel, side), out_shape=pltpu.VMEM((tot...]
where the time goes in v2:
time: 197 us
  Pallas kernels  197 us (100%)
    pallas_call x1, Pallas kernels, step(): pl.pallas_call(functools.partial(kernel, side), out_shape=pltpu.VMEM((tot...  191 us
    pallas_call x1, Pallas kernels, step(): pl.pallas_call(functools.partial(write, per), out_shape=jax.ShapeDtypeStr...  5.92 us

profile of v2, /device:TPU:96, one launch (start us, length us, event | category | flops | bytes accessed | tf_op | source)
XLA Modules:
  0.0 196.7 jit_solution(17630716177481732508)
XLA Ops:
  0.0 190.8 %shard_map.28.sums = bf16[25,640,512]{2,1,0:T(8,128)(2,1)S(1)} custom-call(bf16[4,4096,640]{2,1,0:T(8,128)(2,1)} %bitcast.2, bf16[4,4096,3200]{2,1,0:T(8,128)(2,1)} %bitcast.1.g_hbm), custom_call_target="tpu_custom_call" | custom-call | tf_op jit(solution)/shard_map/pallas_call | solution.py:385
  190.8 5.9 %shard_map.29 = bf16[4,640,3200]{2,1,0:T(8,128)(2,1)} custom-call(bf16[25,640,512]{2,1,0:T(8,128)(2,1)S(1)} %shard_map.28.sums), custom_call_target="tpu_custom_call" | custom-call | tf_op jit(solution)/shard_map/pallas_call | solution.py:417

commit v3 on v2

--- a/solution.py
+++ b/solution.py
@@ -15,6 +15,8 @@
 SENT = 2
 PARTS = 8
 AHEAD = 3
+ORDER = (0, 1, 'D', 2, 3, 4, 5, 'X', 7, 6, 'D', 8)
+LAG = (0, 1, 2, 3, 4, 5, 6, 8, 9)
 BF = jnp.bfloat16
 F32 = jnp.float32
 
@@ -290,6 +292,8 @@
         def _():
             f(t - s)
 
+    steps = (step0, step1, step2, step3, step4, step5, step6, step7, step8)
+
     def turn(t, carry):
         u = t + 1
         n, c = u // per, u % per
@@ -300,51 +304,48 @@
                 for d in range(2):
                     pl.semaphore_wait(credit.at[axis, d], 1)
 
-        stage(t, 0, step0)
-        stage(t, 1, step1)
-
-        @pl.when(u < whole)
-        def _():
-            @pl.when(c == 0)
+        def product(h, first, last):
+            @pl.when(u < whole)
             def _():
-                load_a(n).wait()
-
-            load_g(u).wait()
-            acc[u % ACC, :, pl.ds(0, hc)] = dot(n, gbuf[u % 2, :, pl.ds(0, hc)])
-
-        stage(t, 2, step2)
-        stage(t, 3, step3)
-        stage(t, 4, step4)
-
-        @pl.when(u < whole)
-        def _():
-            acc[u % ACC, :, pl.ds(hc, hc)] = dot(n, gbuf[u % 2, :, pl.ds(hc, hc)])
-
-            @pl.when(u + 2 < whole)
+                if first:
+                    @pl.when(c == 0)
+                    def _():
+                        load_a(n).wait()
+
+                    load_g(u).wait()
+                lanes = pl.ds(h * hc, hc)
+                acc[u % ACC, :, lanes] = dot(n, gbuf[u % 2, :, lanes])
+                if last:
+                    @pl.when(u + 2 < whole)
+                    def _():
+                        load_g(u + 2).start()
+
+        def odd():
+            @pl.when((c == 0) & (u <= whole))
             def _():
-                load_g(u + 2).start()
-
-        stage(t, 5, step5)
-        stage(t, 6, step6)
-
-        @pl.when((c == 0) & (u <= whole))
-        def _():
-            load_x(n - 1).wait()
-            acc[ACC, :, pl.ds(lane0(n - 1), LANE)] = dot(n - 1, xbuf[...])
-
-            @pl.when(n < mats)
-            def _():
-                load_x(n).start()
-
-            @pl.when(n + 1 < mats)
-            def _():
-                load_a(n + 1).start()
-
-        stage(t, 7, step7)
-        stage(t, 8, step8)
+                load_x(n - 1).wait()
+                acc[ACC, :, pl.ds(lane0(n - 1), LANE)] = dot(n - 1, xbuf[...])
+
+                @pl.when(n < mats)
+                def _():
+                    load_x(n).start()
+
+                @pl.when(n + 1 < mats)
+                def _():
+                    load_a(n + 1).start()
+
+        done = 0
+        for item in ORDER:
+            if item == "D":
+                product(done, done == 0, done == 1)
+                done += 1
+            elif item == "X":
+                odd()
+            else:
+                stage(t, LAG[item], steps[item])
         return carry
 
-    lax.fori_loop(0, total + 8, turn, 0)
+    lax.fori_loop(0, total + LAG[8], turn, 0)
 
     for s in range(8):
         for c in range(2):

time: 197 us -> 196 us (level)
  Pallas kernels: 197 us -> 195 us
where the time goes in v3:
time: 196 us; the launch traced here: 195 us
  Pallas kernels  195 us (99%)
    pallas_call x1, Pallas kernels, step(): pl.pallas_call(functools.partial(kernel, side), out_shape=pltpu.VMEM((tot...  189 us
    pallas_call x1, Pallas kernels, step(): pl.pallas_call(functools.partial(write, per), out_shape=jax.ShapeDtypeStr...  5.92 us

profile of v3, /device:TPU:96, one launch (start us, length us, event | category | flops | bytes accessed | tf_op | source)
XLA Modules:
  0.0 195.4 jit_solution(14763757486960913049)
XLA Ops:
  0.0 189.5 %shard_map.28.sums = bf16[25,640,512]{2,1,0:T(8,128)(2,1)S(1)} custom-call(bf16[4,4096,640]{2,1,0:T(8,128)(2,1)} %bitcast.2, bf16[4,4096,3200]{2,1,0:T(8,128)(2,1)} %bitcast.1.g_hbm), custom_call_target="tpu_custom_call" | custom-call | tf_op jit(solution)/shard_map/pallas_call | solution.py:386
  189.5 5.9 %shard_map.29 = bf16[4,640,3200]{2,1,0:T(8,128)(2,1)} custom-call(bf16[25,640,512]{2,1,0:T(8,128)(2,1)S(1)} %shard_map.28.sums), custom_call_target="tpu_custom_call" | custom-call | tf_op jit(solution)/shard_map/pallas_call | solution.py:418
